TPU v7x, 128 devices: a whole 4x4x4 slice. The times are simulated.
128 devices in a mesh: scen: 32 (over x, z, core), blk: 4 (over y).
Axes of the slice: x: 4, y: 4, z: 4, core: 2. Of those that a mesh axis runs over, the one named last changes fastest.
Arguments:
- cons_matrix: bfloat16 [2048, 4096], P(None, 'blk'), may hold values from -0.09375 to 0.09375
- row_scale: float32 [2048, 2048], P('scen'), may hold values from 0.5 to 2
- rhs: float32 [2048, 2048], P('scen'), may hold values from -6 to 6
- cons_mult: float32 [2048, 2048], P('scen'), may hold values from -3 to 3
- cost: float32 [2048, 4096], P('scen', 'blk'), may hold values from -6 to 6
- ph_mult: float32 [2048, 4096], P('scen', 'blk'), may hold values from -3 to 3
- start: float32 [2048, 4096], P('scen', 'blk'), may hold values from -3 to 3
- consensus: float32 [4096], P('blk'), may hold values from -3 to 3
- upper: float32 [4096], P('blk'), may hold values from 0.3 to 1.5
- prob: float32 [2048], P('scen'), may hold values from 1 to 30, as said below
Outputs:
- solutions: float32 [2048, 4096], P('scen', 'blk')
- mult_new: float32 [2048, 2048], P('scen', 'blk')
- z_new: float32 [4096], P('blk')
- w_new: float32 [2048, 4096], P('scen', 'blk')
- primal_res: float32 [], replicated
- dual_res: float32 [], replicated
Inputs may be any that keep to these rules, and one draw needn't show every extreme that they name: prob is positive.
All inputs are finite; a program needn't handle non-finite values.
Results may differ from a plain program's by a relative error of at most 0.0017.
Values may be sent and summed in bfloat16 or wider, within the bound.
No kernel may reach another device: no remote copies, remote signals or barrier semaphores. Data moves between devices by JAX's collectives and lax.ppermute only.
A program may use at most 64 MiB of HBM per device.

v0:
```python
import jax
import jax.numpy as jnp
from jax import lax
from jax.experimental import pallas as pl
from jax.experimental.pallas import tpu as pltpu
from jax.sharding import Mesh
from jax.sharding import PartitionSpec as P


ITERS = 8
penalty = 1.0
aug_weight = 1.0
step_size = 0.05
eps = 1e-06


SCEN = ("x", "z", "c")
ALL = ("x", "z", "c", "y")
RING = 4
TILE = 256


def pairs(move):
    def flat(x, z, c, y):
        return ((x * RING + z) * 2 + c) * RING + y

    spots = [
        (x, z, c, y) for x in range(RING) for z in range(RING) for c in range(2) for y in range(RING)
    ]
    return [(flat(*spot), flat(*move(*spot))) for spot in spots]


def along(step):
    def move(x, z, c, y):
        return ((x + step) % RING, z, c, y) if c == 0 else (x, (z + step) % RING, c, y)

    return pairs(move)


FIRST = pairs(lambda x, z, c, y: (x, z, c, y ^ 1 if c == 0 else 3 - y))
SECOND = pairs(lambda x, z, c, y: (x, z, c, 3 - y if c == 0 else y ^ 1))
OTHER = pairs(lambda x, z, c, y: (x, z, 1 - c, y))
UP, DOWN = along(1), along(-1)


def send(value, perm):
    return lax.ppermute(value, ALL, perm)


def ring_place():
    x, z, c = lax.axis_index("x"), lax.axis_index("z"), lax.axis_index("c")
    return c, jnp.where(c == 0, x, z), jnp.where(c == 0, z, x)


def gather_matrix(matrix, far):
    c, i, _ = ring_place()
    half = matrix.shape[0] // 2
    quarter = half // RING
    own = lax.dynamic_slice_in_dim(matrix, c * half + i * quarter, quarter, 0)
    one = send(own, FIRST)
    three = send(one, SECOND)
    two = send(own, SECOND)
    up1, down1 = send(one, UP), send(one, DOWN)
    up3, down3 = send(three, UP), send(three, DOWN)
    up2, down2 = send(two, UP), send(two, DOWN)
    far1 = send(up1, UP)
    far2 = send(far, SECOND)
    far3 = send(down3, DOWN)
    mine = [[one, up1, down1, far1], [two, up2, down2, far2], [three, up3, down3, far3]]
    theirs = [[send(piece, OTHER) for piece in block] for block in mine]
    return mine, theirs


def prepare(place, cost_h, ph_h, start_h, consensus, upper, matrix, sent, far, cost, ph_mult, start, sem):
    loads = ((cost_h, cost), (ph_h, ph_mult), (start_h, start))
    loads += ((matrix.at[pl.ds(pl.multiple_of(place[3], TILE), TILE)], far),)
    copies = [pltpu.make_async_copy(src, dst, sem.at[k]) for k, (src, dst) in enumerate(loads)]
    for copy in copies:
        copy.start()
    blocks, rows, width = sent.shape
    own = (rows - 8) // 2
    flat = jnp.concatenate([upper[...], consensus[...], jnp.zeros((6, width), jnp.float32)], axis=0)
    for b in range(blocks):
        sent[b, 2 * own :] = flat
    for copy in copies[:3]:
        copy.wait()
    for b in range(blocks):
        at = slice(b * own, (b + 1) * own)
        sent[b, :own] = cost[at] + ph_mult[at] - penalty * consensus[...]
        sent[b, own : 2 * own] = start[at]
    copies[3].wait()


def run_prepare(place, cost, ph_mult, start, consensus, upper, matrix, blocks):
    group, width = start.shape
    vmem = pl.BlockSpec(memory_space=pltpu.VMEM)
    hbm = pl.BlockSpec(memory_space=pltpu.HBM)
    held = pltpu.VMEM((group, width), jnp.float32)
    return pl.pallas_call(
        prepare,
        out_shape=(
            jax.ShapeDtypeStruct((blocks, 2 * group // blocks + 8, width), jnp.float32),
            jax.ShapeDtypeStruct((TILE, width), jnp.bfloat16),
        ),
        in_specs=[pl.BlockSpec(memory_space=pltpu.SMEM)] + [hbm] * 3 + [vmem] * 2 + [hbm],
        out_specs=(vmem, vmem),
        scratch_shapes=[held, held, held, pltpu.SemaphoreType.DMA((4,))],
        compiler_params=pltpu.CompilerParams(vmem_limit_bytes=8 * 1024 * 1024),
        cost_estimate=pl.CostEstimate(
            flops=4000000, bytes_accessed=5 * group * width * 4, transcendentals=0
        ),
        name="prepare",
    )(place, cost, ph_mult, start, consensus[None], upper[None], matrix)


def finish(place, p0, p1, p2, p3, back, ph_mult, old, x, mult, z, w, primal, dual):
    blocks, own, _ = back.shape
    width = x.shape[1]
    n_vars = blocks * width
    parts = (p0[...] + p2[...]) + (p1[...] + p3[...])
    total, square = parts[blocks : blocks + 1, :1], parts[blocks + 1 : blocks + 2, :1]
    z_all = parts[:blocks] / total
    primal_sum = square - total * jnp.sum(z_all * z_all, keepdims=True)
    primal[...] = jnp.sqrt(primal_sum / (total * n_vars) + eps)
    gap = z_all - old[...]
    dual[...] = penalty * jnp.sqrt(jnp.sum(gap * gap, keepdims=True) / n_vars + eps)
    mine = lax.broadcasted_iota(jnp.int32, (blocks, 1), 0) == place[8]
    z_own = jnp.sum(jnp.where(mine, z_all, 0.0), axis=0, keepdims=True)
    z[...] = z_own
    for b in range(blocks):
        at = slice(b * own, (b + 1) * own)
        solved = back[b, :, :width]
        x[at] = solved
        mult[at] = back[b, :, width:]
        w[at] = ph_mult[at] + penalty * (solved - z_own)


def run_finish(place, shares, back, ph_mult, old):
    _, _, both = back.shape
    group, width = ph_mult.shape
    vmem = pl.BlockSpec(memory_space=pltpu.VMEM)
    shapes = ((group, width), (group, both - width), (1, width), (group, width), (1, 1), (1, 1))
    return pl.pallas_call(
        finish,
        out_shape=tuple(jax.ShapeDtypeStruct(shape, jnp.float32) for shape in shapes),
        in_specs=[pl.BlockSpec(memory_space=pltpu.SMEM)] + [vmem] * 7,
        out_specs=(vmem,) * 6,
        compiler_params=pltpu.CompilerParams(vmem_limit_bytes=8 * 1024 * 1024),
        cost_estimate=pl.CostEstimate(
            flops=4000000, bytes_accessed=5 * group * width * 4, transcendentals=0
        ),
        name="finish",
    )(place, *shares, back, ph_mult, old)


def local_steps(place, *refs):
    pieces, refs = refs[:24], refs[24:]
    own_a, scale_h, rhs_h, mult_h, weight_h, state, out, parts = refs[:8]
    a_v, at_v, x_v, w_v, back_v, scale, rhs, mult, weight, sem, row_sem = refs[8:]
    slots, width = a_v.shape[1], a_v.shape[3]
    n_piece = a_v.shape[0]
    rows = n_piece * TILE
    own = x_v.shape[1]
    first = pl.multiple_of(place[12], 8)

    def offset(p):
        return pl.multiple_of(place[p], TILE)

    waits = []
    for p in range(n_piece):
        at = pl.ds(p * TILE, TILE)
        for k, (src, dst) in enumerate(((scale_h, scale), (rhs_h, rhs), (mult_h, mult))):
            copy = pltpu.make_async_copy(
                src.at[pl.ds(first, own), pl.ds(offset(p), TILE)], dst.at[:, at], row_sem.at[p * 3 + k]
            )
            copy.start()
            waits.append(copy)
    copy = pltpu.make_async_copy(weight_h.at[pl.ds(first, own)], weight, row_sem.at[3 * n_piece])
    copy.start()
    waits.append(copy)

    per_half = n_piece // 2
    for p in range(n_piece):
        pltpu.make_async_copy(own_a.at[pl.ds(offset(p), TILE)], a_v.at[p, 0], sem.at[p]).start()
        side, q = divmod(p, per_half)
        for k in range(3):
            slot = 1 + (k if side == 0 else (1, 0, 2)[k])
            piece = pieces[side * 12 + k * 4 + q]
            pltpu.make_async_copy(piece, a_v.at[p, slot], sem.at[p]).start()

    for b in range(slots):
        x_v[b] = state[place[8 + b], own : 2 * own]
    for copy in waits:
        copy.wait()

    def turned(p):
        pltpu.make_async_copy(a_v.at[p], a_v.at[p], sem.at[p]).wait()
        at = pl.ds(pl.multiple_of(p * TILE, TILE), TILE)
        for b in range(slots):
            for j in range(width // TILE):
                var = b * width + j * TILE
                at_v[var : var + TILE, at] = a_v[p, b, :, j * TILE : (j + 1) * TILE].T

    def current():
        return jnp.concatenate([x_v[b] for b in range(slots)], axis=1).astype(jnp.bfloat16)

    def residual(p, xb):
        at = pl.ds(pl.multiple_of(p * TILE, TILE), TILE)
        prod = jnp.dot(xb, at_v[:, at], preferred_element_type=jnp.float32)
        return mult[:, at] + aug_weight * (scale[:, at] * prod - rhs[:, at])

    def weigh(p, xb):
        at = pl.ds(pl.multiple_of(p * TILE, TILE), TILE)
        w_v[:, at] = (scale[:, at] * residual(p, xb)).astype(jnp.bfloat16)

    def add_back(p):
        at = pl.ds(pl.multiple_of(p * TILE, TILE), TILE)
        for b in range(slots):
            for j in range(width // TILE):
                col = slice(j * TILE, (j + 1) * TILE)
                back_v[b, :, col] += jnp.dot(
                    w_v[:, at], a_v[p, b, :, col], preferred_element_type=jnp.float32
                )

    def move(b, col, back):
        block = place[8 + b]
        x = x_v[b, :, col]
        grad = state[block, :own, col] + penalty * x + back
        box = state[block, 2 * own : 2 * own + 1, col]
        x_v[b, :, col] = jnp.clip(x - step_size * grad, -box, box)

    back_v[...] = jnp.zeros_like(back_v)
    turned(0)
    weigh(0, current())

    @pl.loop(1, n_piece)
    def _(p):
        turned(p)
        add_back(p - 1)
        weigh(p, current())

    add_back(n_piece - 1)
    for b in range(slots):
        for j in range(width // TILE):
            col = slice(j * TILE, (j + 1) * TILE)
            move(b, col, back_v[b, :, col])

    @pl.loop(1, ITERS)
    def _(i):
        xb = current()
        for p in range(n_piece):
            weigh(p, xb)
        w = w_v[...]
        for b in range(slots):
            for j in range(width // TILE):
                col = slice(j * TILE, (j + 1) * TILE)
                tall = a_v[:, b, :, col].reshape(rows, TILE)
                move(b, col, jnp.dot(w, tall, preferred_element_type=jnp.float32))

    share = rows // slots
    xb = current()
    for p in range(n_piece):
        at = place[p]
        inside = pl.ds(pl.multiple_of(width + lax.rem(at, share), TILE), TILE)
        out[lax.div(at, share), :, inside] = residual(p, xb)
    square = jnp.zeros((1, 1), jnp.float32)
    for b in range(slots):
        block = place[8 + b]
        x = x_v[b]
        out[block, :, :width] = x
        weighted = weight[:, :1] * x
        parts[pl.ds(block, 1), :] = jnp.sum(weighted, axis=0, keepdims=True)
        square += jnp.sum(weighted * x, keepdims=True)
    total = jnp.sum(weight[:, :1], axis=0, keepdims=True)
    parts[4:5, :] = jnp.broadcast_to(total, (1, width))
    parts[5:6, :] = jnp.broadcast_to(square, (1, width))
    parts[6:8, :] = jnp.zeros((2, width), jnp.float32)


def run_local(place, mine, theirs, matrix, scale, rhs, mult, weight, state):
    rows, width = matrix.shape
    blocks = state.shape[0]
    own = scale.shape[0] // blocks
    n_piece = rows // TILE
    pieces = [piece for block in mine + theirs for piece in block]
    vmem = pl.BlockSpec(memory_space=pltpu.VMEM)
    hbm = pl.BlockSpec(memory_space=pltpu.HBM)
    smem = pl.BlockSpec(memory_space=pltpu.SMEM)
    per_row = pltpu.VMEM((own, rows), jnp.float32)
    return pl.pallas_call(
        local_steps,
        out_shape=(
            jax.ShapeDtypeStruct((blocks, own, width + rows // blocks), jnp.float32),
            jax.ShapeDtypeStruct((8, width), jnp.float32),
        ),
        in_specs=[smem] + [hbm] * (len(pieces) + 5) + [vmem],
        out_specs=(vmem, vmem),
        scratch_shapes=[
            pltpu.VMEM((n_piece, blocks, TILE, width), jnp.bfloat16),
            pltpu.VMEM((blocks * width, rows), jnp.bfloat16),
            pltpu.VMEM((blocks, own, width), jnp.float32),
            pltpu.VMEM((own, rows), jnp.bfloat16),
            pltpu.VMEM((blocks, own, width), jnp.float32),
            per_row,
            per_row,
            per_row,
            pltpu.VMEM((own, 128), jnp.float32),
            pltpu.SemaphoreType.DMA((n_piece,)),
            pltpu.SemaphoreType.DMA((3 * n_piece + 1,)),
        ],
        compiler_params=pltpu.CompilerParams(vmem_limit_bytes=44 * 1024 * 1024),
        cost_estimate=pl.CostEstimate(
            flops=2 * (2 * ITERS + 1) * own * rows * blocks * width,
            bytes_accessed=2 * blocks * rows * width,
            transcendentals=0,
        ),
        name="local_steps",
    )(place, *pieces, matrix, scale, rhs, mult, weight, state)


def shift(value, axis, by):
    n = lax.axis_size(axis)
    return lax.ppermute(value, axis, [(i, (i + by) % n) for i in range(n)])


def ring_sum(value, axis):
    return (value + shift(value, axis, 2)) + (shift(value, axis, 1) + shift(value, axis, 3))


def per_device(cons_matrix, row_scale, rhs, cons_mult, cost, ph_mult, start, consensus, upper, prob):
    blocks = lax.axis_size("y")
    me = lax.axis_index("y")
    rows, _ = cons_matrix.shape
    group = start.shape[0]
    own = group // blocks

    c, i, j = ring_place()
    half = rows // 2
    turn = jnp.array([0, 3, 1, 2], jnp.int32)
    near, far = me ^ 1, 3 - me
    place = jnp.concatenate(
        [
            c * half + (i + turn) % RING * TILE,
            (1 - c) * half + (j + turn) % RING * TILE,
            jnp.stack([me, jnp.where(c == 0, near, far), jnp.where(c == 0, far, near), me ^ 2]),
            jnp.stack([me * own]),
        ]
    ).astype(jnp.int32)
    sent, far = run_prepare(place, cost, ph_mult, start, consensus, upper, cons_matrix, blocks)
    mine, theirs = gather_matrix(cons_matrix, far)
    state = lax.all_to_all(sent, "y", 0, 0, tiled=True)

    weight = jnp.broadcast_to(prob[:, None], (group, 128))
    result, parts = run_local(
        place, mine, theirs, cons_matrix, row_scale, rhs, cons_mult, weight, state
    )

    back = lax.all_to_all(result, "y", 0, 0, tiled=True)
    parts = parts + send(parts, OTHER)
    parts = ring_sum(ring_sum(parts, "x"), "z")
    shares = (parts, shift(parts, "y", 1), shift(parts, "y", 2), shift(parts, "y", 3))
    x, mult_new, z_new, w_new, primal_res, dual_res = run_finish(
        place, shares, back, ph_mult, state[:, 2 * own + 1]
    )
    return (x, mult_new, z_new[0], w_new, primal_res[0, 0], dual_res[0, 0])


def solution(mesh):
    fine = Mesh(mesh.devices.reshape(RING, RING, 2, RING), ALL)
    in_specs = (
        P(None, "y"),
        P(SCEN, None),
        P(SCEN, None),
        P(SCEN, None),
        P(SCEN, "y"),
        P(SCEN, "y"),
        P(SCEN, "y"),
        P("y"),
        P("y"),
        P(SCEN),
    )
    out_specs = (P(SCEN, "y"), P(SCEN, "y"), P("y"), P(SCEN, "y"), P(), P())
    return jax.shard_map(per_device, mesh=fine, in_specs=in_specs, out_specs=out_specs, check_vma=False)
```

profile of v0, /device:TPU:0, one launch (start us, length us, event | category | flops | bytes accessed | tf_op | source)
XLA Modules:
  0.0 157.2 jit_solution(16950021568134775051)
XLA Ops:
  1.4 2.2 %copy-done = bf16[2048,1024]{1,0:T(8,128)(2,1)S(1)} copy-done((bf16[2048,1024]{1,0:T(8,128)(2,1)S(1)}, bf16[2048,1024]{1,0:T(8,128)(2,1)}, u32[]{:S(2)}) %copy-start) | copy-done | bytes 4194328
  8.6 3.2 %collective-permute-start.7 = (bf16[256,1024]{1,0:T(8,128)(2,1)S(1)}, bf16[256,1024]{1,0:T(8,128)(2,1)S(1)}, u32[]{:S(2)}, u32[]{:S(2)}) collective-permute-start(bf16[256,1024]{1,0:T(8,128)(2,1)S(1)} %get-tuple-element.16), channel_id=1, source_target_pairs={{0,3},{1,2},{2,1},{3,0},{4,5},{5,4},{6,7},{7,6},{8,11},{9,10},{10,... | collective-permute-start | bytes 1572872 | tf_op jit(solution)/shard_map/ppermute | solution.py:47
  11.8 1.1 constant_dynamic-slice_fusion
  13.1 1.1 collective-permute-start.4
  14.1 9.5 %collective-permute-done.7.refs_7_ = bf16[256,1024]{1,0:T(8,128)(2,1)S(1)} collective-permute-done((bf16[256,1024]{1,0:T(8,128)(2,1)S(1)}, bf16[256,1024]{1,0:T(8,128)(2,1)S(1)}, u32[]{:S(2)}, u32[]{:S(2)}) %collective-permute-start.7) | collective-permute-done | bytes 524320 | tf_op jit(solution)/shard_map/ppermute | solution.py:47
  23.6 4.1 %collective-permute-done.refs_0_ = bf16[256,1024]{1,0:T(8,128)(2,1)S(1)} collective-permute-done((bf16[256,1024]{1,0:T(8,128)(2,1)S(1)}, bf16[256,1024]{1,0:T(8,128)(2,1)S(1)}, u32[]{:S(2)}, u32[]{:S(2)}) %collective-permute-start) | collective-permute-done | bytes 524320 | tf_op jit(solution)/shard_map/ppermute | solution.py:47
  27.9 1.6 %collective-permute-start.1 = (bf16[256,1024]{1,0:T(8,128)(2,1)S(1)}, bf16[256,1024]{1,0:T(8,128)(2,1)S(1)}, u32[]{:S(2)}, u32[]{:S(2)}) collective-permute-start(bf16[256,1024]{1,0:T(8,128)(2,1)S(1)} %collective-permute-done.refs_0_), channel_id=1, source_target_pairs={{0,32},{1,33},{2,34},{3,35},{4,12},{5,13},{6,14},{7,15},{8,40},{9,... | collective-permute-start | bytes 1572872 | tf_op jit(solution)/shard_map/ppermute | solution.py:47
  29.5 1.6 %collective-permute-start.2 = (bf16[256,1024]{1,0:T(8,128)(2,1)S(1)}, bf16[256,1024]{1,0:T(8,128)(2,1)S(1)}, u32[]{:S(2)}, u32[]{:S(2)}) collective-permute-start(bf16[256,1024]{1,0:T(8,128)(2,1)S(1)} %collective-permute-done.refs_0_), channel_id=1, source_target_pairs={{0,96},{1,97},{2,98},{3,99},{4,28},{5,29},{6,30},{7,31},{8,104},{9... | collective-permute-start | bytes 1572872 | tf_op jit(solution)/shard_map/ppermute | solution.py:47
  31.9 2.4 %collective-permute-start.6 = (bf16[256,1024]{1,0:T(8,128)(2,1)S(1)}, bf16[256,1024]{1,0:T(8,128)(2,1)S(1)}, u32[]{:S(2)}, u32[]{:S(2)}) collective-permute-start(bf16[256,1024]{1,0:T(8,128)(2,1)S(1)} %collective-permute-done.4.refs_4_), channel_id=1, source_target_pairs={{0,96},{1,97},{2,98},{3,99},{4,28},{5,29},{6,30},{7,31},{8,104},{9... | collective-permute-start | bytes 1572872 | tf_op jit(solution)/shard_map/ppermute | solution.py:47
  34.3 3.8 %collective-permute-done.8.refs_8_ = bf16[256,1024]{1,0:T(8,128)(2,1)S(1)} collective-permute-done((bf16[256,1024]{1,0:T(8,128)(2,1)S(1)}, bf16[256,1024]{1,0:T(8,128)(2,1)S(1)}, u32[]{:S(2)}, u32[]{:S(2)}) %collective-permute-start.8) | collective-permute-done | bytes 524320 | tf_op jit(solution)/shard_map/ppermute | solution.py:47
  38.6 2.8 %collective-permute-start.10 = (bf16[256,1024]{1,0:T(8,128)(2,1)S(1)}, bf16[256,1024]{1,0:T(8,128)(2,1)S(1)}, u32[]{:S(2)}, u32[]{:S(2)}) collective-permute-start(bf16[256,1024]{1,0:T(8,128)(2,1)S(1)} %collective-permute-done.8.refs_8_), channel_id=1, source_target_pairs={{0,96},{1,97},{2,98},{3,99},{4,28},{5,29},{6,30},{7,31},{8,104},{9... | collective-permute-start | bytes 1572872 | tf_op jit(solution)/shard_map/ppermute | solution.py:47
  41.5 2.4 %collective-permute-done.5.refs_5_ = bf16[256,1024]{1,0:T(8,128)(2,1)S(1)} collective-permute-done((bf16[256,1024]{1,0:T(8,128)(2,1)S(1)}, bf16[256,1024]{1,0:T(8,128)(2,1)S(1)}, u32[]{:S(2)}, u32[]{:S(2)}) %collective-permute-start.5) | collective-permute-done | bytes 524320 | tf_op jit(solution)/shard_map/ppermute | solution.py:47
  44.3 1.5 collective-permute-start.3
  46.3 3.6 %collective-permute-done.10.refs_10_ = bf16[256,1024]{1,0:T(8,128)(2,1)S(1)} collective-permute-done((bf16[256,1024]{1,0:T(8,128)(2,1)S(1)}, bf16[256,1024]{1,0:T(8,128)(2,1)S(1)}, u32[]{:S(2)}, u32[]{:S(2)}) %collective-permute-start.10) | collective-permute-done | bytes 524320 | tf_op jit(solution)/shard_map/ppermute | solution.py:47
  49.9 4.4 %collective-permute-done.9.refs_9_ = bf16[256,1024]{1,0:T(8,128)(2,1)S(1)} collective-permute-done((bf16[256,1024]{1,0:T(8,128)(2,1)S(1)}, bf16[256,1024]{1,0:T(8,128)(2,1)S(1)}, u32[]{:S(2)}, u32[]{:S(2)}) %collective-permute-start.9) | collective-permute-done | bytes 524320 | tf_op jit(solution)/shard_map/ppermute | solution.py:47
  54.3 5.6 %collective-permute-done.3.refs_3_ = bf16[256,1024]{1,0:T(8,128)(2,1)S(1)} collective-permute-done((bf16[256,1024]{1,0:T(8,128)(2,1)S(1)}, bf16[256,1024]{1,0:T(8,128)(2,1)S(1)}, u32[]{:S(2)}, u32[]{:S(2)}) %collective-permute-start.3) | collective-permute-done | bytes 524320 | tf_op jit(solution)/shard_map/ppermute | solution.py:47
  61.4 7.7 %collective-permute-done.11.refs_11_ = bf16[256,1024]{1,0:T(8,128)(2,1)S(1)} collective-permute-done((bf16[256,1024]{1,0:T(8,128)(2,1)S(1)}, bf16[256,1024]{1,0:T(8,128)(2,1)S(1)}, u32[]{:S(2)}, u32[]{:S(2)}) %collective-permute-start.11) | collective-permute-done | bytes 524320 | tf_op jit(solution)/shard_map/ppermute | solution.py:47
  69.1 15.8 %all_to_all.10.refs_29_ = f32[4,40,1024]{2,1,0:T(8,128)} all-to-all(f32[4,40,1024]{2,1,0:T(8,128)S(1)} %get-tuple-element.17), channel_id=1, replica_groups=mesh['x'=4,'z'=4,'c'=2,'y'=4] {'y'}, dimensions={0} | all-to-all | bytes 1310720 | tf_op jit(solution)/shard_map/all_to_all | solution.py:351
  86.2 43.2 %local_steps.1 = (f32[4,16,1536]{2,1,0:T(8,128)}, f32[8,1024]{1,0:T(8,128)S(1)}) custom-call(s32[13]{0:T(128)S(1)} %concatenate.3.place, bf16[256,1024]{1,0:T(8,128)(2,1)S(1)} %collective-permute-done.refs_0_, bf16[256,1024]{1,0:T(8,128)(2,1)S(1)} %collective-permute-done.1.refs_1_, bf16[256,1024]{1,0:T(8,128)(2,1)S(1)} %collective-permute-done.2.refs_2_, ...), custom_call_target="tpu_custom_call" | custom-call | flops 4563402752 | bytes 16777216 | tf_op jit(solution)/shard_map/local_steps/pallas_call | solution.py:290
  129.5 1.2 collective-permute-done.24
  131.3 1.8 %collective-permute-start.26 = (f32[8,1024]{1,0:T(8,128)S(1)}, f32[8,1024]{1,0:T(8,128)S(1)}, u32[]{:S(2)}, u32[]{:S(2)}) collective-permute-start(f32[8,1024]{1,0:T(8,128)S(1)} %add.73), channel_id=1, source_target_pairs={{0,32},{32,64},{64,96},{96,0},{1,33},{33,65},{65,97},{97,1},{2,34}... | collective-permute-start | bytes 98312 | tf_op jit(solution)/shard_map/ppermute | solution.py:323
  133.1 1.4 collective-permute-start.27
  134.5 3.5 %all-to-all-start.1 = ((f32[4,16,1536]{2,1,0:T(8,128)}), f32[4,16,1536]{2,1,0:T(8,128)S(1)}, u32[]{:S(2)}, u32[]{:S(2)}) async-start(f32[4,16,1536]{2,1,0:T(8,128)} %get-tuple-element.19), calls=%async_computation.1 | async-start | bytes 786432 | tf_op jit(solution)/shard_map/all_to_all | solution.py:358
  138.0 4.0 %collective-permute-start.28 = (f32[8,1024]{1,0:T(8,128)S(1)}, f32[8,1024]{1,0:T(8,128)S(1)}, u32[]{:S(2)}, u32[]{:S(2)}) collective-permute-start(f32[8,1024]{1,0:T(8,128)S(1)} %add_add_fusion.1), channel_id=1, source_target_pairs={{0,16},{8,24},{16,0},{24,8},{1,17},{9,25},{17,1},{25,9},{2,18},{10... | collective-permute-start | bytes 98312 | tf_op jit(solution)/shard_map/ppermute | solution.py:323
  142.0 1.0 collective-permute-start.29
  143.0 2.2 %collective-permute-start.30 = (f32[8,1024]{1,0:T(8,128)S(1)}, f32[8,1024]{1,0:T(8,128)S(1)}, u32[]{:S(2)}, u32[]{:S(2)}) collective-permute-start(f32[8,1024]{1,0:T(8,128)S(1)} %add_add_fusion.1), channel_id=1, source_target_pairs={{0,24},{8,0},{16,8},{24,16},{1,25},{9,1},{17,9},{25,17},{2,26},{10... | collective-permute-start | bytes 98312 | tf_op jit(solution)/shard_map/ppermute | solution.py:323
  145.2 1.9 %collective-permute-done.29 = f32[8,1024]{1,0:T(8,128)S(1)} collective-permute-done((f32[8,1024]{1,0:T(8,128)S(1)}, f32[8,1024]{1,0:T(8,128)S(1)}, u32[]{:S(2)}, u32[]{:S(2)}) %collective-permute-start.29) | collective-permute-done | bytes 32800 | tf_op jit(solution)/shard_map/ppermute | solution.py:323
  147.1 2.0 %collective-permute-start.31 = (f32[8,1024]{1,0:T(8,128)S(1)}, f32[8,1024]{1,0:T(8,128)S(1)}, u32[]{:S(2)}, u32[]{:S(2)}) collective-permute-start(f32[8,1024]{1,0:T(8,128)S(1)} %add_add_fusion.p0), channel_id=1, source_target_pairs={{0,1},{1,2},{2,3},{3,0},{4,5},{5,6},{6,7},{7,4},{8,9},{9,10},{10,1... | collective-permute-start | bytes 98312 | tf_op jit(solution)/shard_map/ppermute | solution.py:323
  149.2 2.7 %collective-permute-start.32 = (f32[8,1024]{1,0:T(8,128)S(1)}, f32[8,1024]{1,0:T(8,128)S(1)}, u32[]{:S(2)}, u32[]{:S(2)}) collective-permute-start(f32[8,1024]{1,0:T(8,128)S(1)} %add_add_fusion.p0), channel_id=1, source_target_pairs={{0,2},{1,3},{2,0},{3,1},{4,6},{5,7},{6,4},{7,5},{8,10},{9,11},{10,... | collective-permute-start | bytes 98312 | tf_op jit(solution)/shard_map/ppermute | solution.py:323
  151.9 1.5 collective-permute-start.33
  154.6 1.2 collective-permute-done.33.p3
  155.8 1.4 finish.1
  (79 shorter events, 13.0 us)
Async XLA Ops:
  8.6 15.0 %collective-permute-start.7 = (bf16[256,1024]{1,0:T(8,128)(2,1)S(1)}, bf16[256,1024]{1,0:T(8,128)(2,1)S(1)}, u32[]{:S(2)}, u32[]{:S(2)}) collective-permute-start(bf16[256,1024]{1,0:T(8,128)(2,1)S(1)} %get-tuple-element.16), channel_id=1, source_target_pairs={{0,3},{1,2},{2,1},{3,0},{4,5},{5,4},{6,7},{7,6},{8,11},{9,10},{10,... | collective-permute-start | bytes 1572872 | tf_op jit(solution)/shard_map/ppermute | solution.py:47
  12.9 14.9 %collective-permute-start = (bf16[256,1024]{1,0:T(8,128)(2,1)S(1)}, bf16[256,1024]{1,0:T(8,128)(2,1)S(1)}, u32[]{:S(2)}, u32[]{:S(2)}) collective-permute-start(bf16[256,1024]{1,0:T(8,128)(2,1)S(1)} %constant_dynamic-slice_fusion), channel_id=1, source_target_pairs={{0,1},{1,0},{2,3},{3,2},{4,7},{5,6},{6,5},{7,4},{8,9},{9,8},{10,11... | collective-permute-start | bytes 1572872 | tf_op jit(solution)/shard_map/ppermute | solution.py:47
  13.1 18.0 %collective-permute-start.4 = (bf16[256,1024]{1,0:T(8,128)(2,1)S(1)}, bf16[256,1024]{1,0:T(8,128)(2,1)S(1)}, u32[]{:S(2)}, u32[]{:S(2)}) collective-permute-start(bf16[256,1024]{1,0:T(8,128)(2,1)S(1)} %constant_dynamic-slice_fusion), channel_id=1, source_target_pairs={{0,3},{1,2},{2,1},{3,0},{4,5},{5,4},{6,7},{7,6},{8,11},{9,10},{10,... | collective-permute-start | bytes 1572872 | tf_op jit(solution)/shard_map/ppermute | solution.py:47
  23.6 8.3 %collective-permute-start.19 = (bf16[256,1024]{1,0:T(8,128)(2,1)S(1)}, bf16[256,1024]{1,0:T(8,128)(2,1)S(1)}, u32[]{:S(2)}, u32[]{:S(2)}) collective-permute-start(bf16[256,1024]{1,0:T(8,128)(2,1)S(1)} %collective-permute-done.7.refs_7_), channel_id=1, source_target_pairs={{0,4},{1,5},{2,6},{3,7},{4,0},{5,1},{6,2},{7,3},{8,12},{9,13},{10,... | collective-permute-start | bytes 1572872 | tf_op jit(solution)/shard_map/ppermute | solution.py:47
  27.7 10.4 %collective-permute-start.8 = (bf16[256,1024]{1,0:T(8,128)(2,1)S(1)}, bf16[256,1024]{1,0:T(8,128)(2,1)S(1)}, u32[]{:S(2)}, u32[]{:S(2)}) collective-permute-start(bf16[256,1024]{1,0:T(8,128)(2,1)S(1)} %collective-permute-done.refs_0_), channel_id=1, source_target_pairs={{0,3},{1,2},{2,1},{3,0},{4,5},{5,4},{6,7},{7,6},{8,11},{9,10},{10,... | collective-permute-start | bytes 1572872 | tf_op jit(solution)/shard_map/ppermute | solution.py:47
  27.9 10.4 %collective-permute-start.1 = (bf16[256,1024]{1,0:T(8,128)(2,1)S(1)}, bf16[256,1024]{1,0:T(8,128)(2,1)S(1)}, u32[]{:S(2)}, u32[]{:S(2)}) collective-permute-start(bf16[256,1024]{1,0:T(8,128)(2,1)S(1)} %collective-permute-done.refs_0_), channel_id=1, source_target_pairs={{0,32},{1,33},{2,34},{3,35},{4,12},{5,13},{6,14},{7,15},{8,40},{9,... | collective-permute-start | bytes 1572872 | tf_op jit(solution)/shard_map/ppermute | solution.py:47
  29.5 9.2 %collective-permute-start.2 = (bf16[256,1024]{1,0:T(8,128)(2,1)S(1)}, bf16[256,1024]{1,0:T(8,128)(2,1)S(1)}, u32[]{:S(2)}, u32[]{:S(2)}) collective-permute-start(bf16[256,1024]{1,0:T(8,128)(2,1)S(1)} %collective-permute-done.refs_0_), channel_id=1, source_target_pairs={{0,96},{1,97},{2,98},{3,99},{4,28},{5,29},{6,30},{7,31},{8,104},{9... | collective-permute-start | bytes 1572872 | tf_op jit(solution)/shard_map/ppermute | solution.py:47
  31.1 12.8 %collective-permute-start.5 = (bf16[256,1024]{1,0:T(8,128)(2,1)S(1)}, bf16[256,1024]{1,0:T(8,128)(2,1)S(1)}, u32[]{:S(2)}, u32[]{:S(2)}) collective-permute-start(bf16[256,1024]{1,0:T(8,128)(2,1)S(1)} %collective-permute-done.4.refs_4_), channel_id=1, source_target_pairs={{0,32},{1,33},{2,34},{3,35},{4,12},{5,13},{6,14},{7,15},{8,40},{9,... | collective-permute-start | bytes 1572872 | tf_op jit(solution)/shard_map/ppermute | solution.py:47
  31.9 12.4 %collective-permute-start.6 = (bf16[256,1024]{1,0:T(8,128)(2,1)S(1)}, bf16[256,1024]{1,0:T(8,128)(2,1)S(1)}, u32[]{:S(2)}, u32[]{:S(2)}) collective-permute-start(bf16[256,1024]{1,0:T(8,128)(2,1)S(1)} %collective-permute-done.4.refs_4_), channel_id=1, source_target_pairs={{0,96},{1,97},{2,98},{3,99},{4,28},{5,29},{6,30},{7,31},{8,104},{9... | collective-permute-start | bytes 1572872 | tf_op jit(solution)/shard_map/ppermute | solution.py:47
  38.1 7.6 %collective-permute-start.12 = (bf16[256,1024]{1,0:T(8,128)(2,1)S(1)}, bf16[256,1024]{1,0:T(8,128)(2,1)S(1)}, u32[]{:S(2)}, u32[]{:S(2)}) collective-permute-start(bf16[256,1024]{1,0:T(8,128)(2,1)S(1)} %collective-permute-done.refs_0_), channel_id=1, source_target_pairs={{0,4},{1,5},{2,6},{3,7},{4,0},{5,1},{6,2},{7,3},{8,12},{9,13},{10,... | collective-permute-start | bytes 1572872 | tf_op jit(solution)/shard_map/ppermute | solution.py:47
  38.2 7.5 %collective-permute-start.16 = (bf16[256,1024]{1,0:T(8,128)(2,1)S(1)}, bf16[256,1024]{1,0:T(8,128)(2,1)S(1)}, u32[]{:S(2)}, u32[]{:S(2)}) collective-permute-start(bf16[256,1024]{1,0:T(8,128)(2,1)S(1)} %collective-permute-done.4.refs_4_), channel_id=1, source_target_pairs={{0,4},{1,5},{2,6},{3,7},{4,0},{5,1},{6,2},{7,3},{8,12},{9,13},{10,... | collective-permute-start | bytes 1572872 | tf_op jit(solution)/shard_map/ppermute | solution.py:47
  38.6 11.2 %collective-permute-start.10 = (bf16[256,1024]{1,0:T(8,128)(2,1)S(1)}, bf16[256,1024]{1,0:T(8,128)(2,1)S(1)}, u32[]{:S(2)}, u32[]{:S(2)}) collective-permute-start(bf16[256,1024]{1,0:T(8,128)(2,1)S(1)} %collective-permute-done.8.refs_8_), channel_id=1, source_target_pairs={{0,96},{1,97},{2,98},{3,99},{4,28},{5,29},{6,30},{7,31},{8,104},{9... | collective-permute-start | bytes 1572872 | tf_op jit(solution)/shard_map/ppermute | solution.py:47
  43.9 10.4 %collective-permute-start.9 = (bf16[256,1024]{1,0:T(8,128)(2,1)S(1)}, bf16[256,1024]{1,0:T(8,128)(2,1)S(1)}, u32[]{:S(2)}, u32[]{:S(2)}) collective-permute-start(bf16[256,1024]{1,0:T(8,128)(2,1)S(1)} %collective-permute-done.8.refs_8_), channel_id=1, source_target_pairs={{0,32},{1,33},{2,34},{3,35},{4,12},{5,13},{6,14},{7,15},{8,40},{9,... | collective-permute-start | bytes 1572872 | tf_op jit(solution)/shard_map/ppermute | solution.py:47
  44.3 15.6 %collective-permute-start.3 = (bf16[256,1024]{1,0:T(8,128)(2,1)S(1)}, bf16[256,1024]{1,0:T(8,128)(2,1)S(1)}, u32[]{:S(2)}, u32[]{:S(2)}) collective-permute-start(bf16[256,1024]{1,0:T(8,128)(2,1)S(1)} %collective-permute-done.1.refs_1_), channel_id=1, source_target_pairs={{0,32},{1,33},{2,34},{3,35},{4,12},{5,13},{6,14},{7,15},{8,40},{9,... | collective-permute-start | bytes 1572872 | tf_op jit(solution)/shard_map/ppermute | solution.py:47
  45.8 14.6 %collective-permute-start.20 = (bf16[256,1024]{1,0:T(8,128)(2,1)S(1)}, bf16[256,1024]{1,0:T(8,128)(2,1)S(1)}, u32[]{:S(2)}, u32[]{:S(2)}) collective-permute-start(bf16[256,1024]{1,0:T(8,128)(2,1)S(1)} %collective-permute-done.8.refs_8_), channel_id=1, source_target_pairs={{0,4},{1,5},{2,6},{3,7},{4,0},{5,1},{6,2},{7,3},{8,12},{9,13},{10,... | collective-permute-start | bytes 1572872 | tf_op jit(solution)/shard_map/ppermute | solution.py:47
  45.8 14.6 %collective-permute-start.13 = (bf16[256,1024]{1,0:T(8,128)(2,1)S(1)}, bf16[256,1024]{1,0:T(8,128)(2,1)S(1)}, u32[]{:S(2)}, u32[]{:S(2)}) collective-permute-start(bf16[256,1024]{1,0:T(8,128)(2,1)S(1)} %collective-permute-done.1.refs_1_), channel_id=1, source_target_pairs={{0,4},{1,5},{2,6},{3,7},{4,0},{5,1},{6,2},{7,3},{8,12},{9,13},{10,... | collective-permute-start | bytes 1572872 | tf_op jit(solution)/shard_map/ppermute | solution.py:47
  49.9 11.0 %collective-permute-start.14 = (bf16[256,1024]{1,0:T(8,128)(2,1)S(1)}, bf16[256,1024]{1,0:T(8,128)(2,1)S(1)}, u32[]{:S(2)}, u32[]{:S(2)}) collective-permute-start(bf16[256,1024]{1,0:T(8,128)(2,1)S(1)} %collective-permute-done.2.refs_2_), channel_id=1, source_target_pairs={{0,4},{1,5},{2,6},{3,7},{4,0},{5,1},{6,2},{7,3},{8,12},{9,13},{10,... | collective-permute-start | bytes 1572872 | tf_op jit(solution)/shard_map/ppermute | solution.py:47
  54.3 6.7 %collective-permute-start.17 = (bf16[256,1024]{1,0:T(8,128)(2,1)S(1)}, bf16[256,1024]{1,0:T(8,128)(2,1)S(1)}, u32[]{:S(2)}, u32[]{:S(2)}) collective-permute-start(bf16[256,1024]{1,0:T(8,128)(2,1)S(1)} %collective-permute-done.5.refs_5_), channel_id=1, source_target_pairs={{0,4},{1,5},{2,6},{3,7},{4,0},{5,1},{6,2},{7,3},{8,12},{9,13},{10,... | collective-permute-start | bytes 1572872 | tf_op jit(solution)/shard_map/ppermute | solution.py:47
  59.9 9.2 %collective-permute-start.11 = (bf16[256,1024]{1,0:T(8,128)(2,1)S(1)}, bf16[256,1024]{1,0:T(8,128)(2,1)S(1)}, u32[]{:S(2)}, u32[]{:S(2)}) collective-permute-start(bf16[256,1024]{1,0:T(8,128)(2,1)S(1)} %collective-permute-done.10.refs_10_), channel_id=1, source_target_pairs={{0,96},{1,97},{2,98},{3,99},{4,28},{5,29},{6,30},{7,31},{8,104},{9... | collective-permute-start | bytes 1572872 | tf_op jit(solution)/shard_map/ppermute | solution.py:47
  60.3 24.6 %collective-permute-start.18 = (bf16[256,1024]{1,0:T(8,128)(2,1)S(1)}, bf16[256,1024]{1,0:T(8,128)(2,1)S(1)}, u32[]{:S(2)}, u32[]{:S(2)}) collective-permute-start(bf16[256,1024]{1,0:T(8,128)(2,1)S(1)} %collective-permute-done.6.refs_6_), channel_id=1, source_target_pairs={{0,4},{1,5},{2,6},{3,7},{4,0},{5,1},{6,2},{7,3},{8,12},{9,13},{10,... | collective-permute-start | bytes 1572872 | tf_op jit(solution)/shard_map/ppermute | solution.py:47
  60.3 24.6 %collective-permute-start.22 = (bf16[256,1024]{1,0:T(8,128)(2,1)S(1)}, bf16[256,1024]{1,0:T(8,128)(2,1)S(1)}, u32[]{:S(2)}, u32[]{:S(2)}) collective-permute-start(bf16[256,1024]{1,0:T(8,128)(2,1)S(1)} %collective-permute-done.10.refs_10_), channel_id=1, source_target_pairs={{0,4},{1,5},{2,6},{3,7},{4,0},{5,1},{6,2},{7,3},{8,12},{9,13},{10,... | collective-permute-start | bytes 1572872 | tf_op jit(solution)/shard_map/ppermute | solution.py:47
  60.8 24.1 %collective-permute-start.21 = (bf16[256,1024]{1,0:T(8,128)(2,1)S(1)}, bf16[256,1024]{1,0:T(8,128)(2,1)S(1)}, u32[]{:S(2)}, u32[]{:S(2)}) collective-permute-start(bf16[256,1024]{1,0:T(8,128)(2,1)S(1)} %collective-permute-done.9.refs_9_), channel_id=1, source_target_pairs={{0,4},{1,5},{2,6},{3,7},{4,0},{5,1},{6,2},{7,3},{8,12},{9,13},{10,... | collective-permute-start | bytes 1572872 | tf_op jit(solution)/shard_map/ppermute | solution.py:47
  60.9 24.0 %collective-permute-start.15 = (bf16[256,1024]{1,0:T(8,128)(2,1)S(1)}, bf16[256,1024]{1,0:T(8,128)(2,1)S(1)}, u32[]{:S(2)}, u32[]{:S(2)}) collective-permute-start(bf16[256,1024]{1,0:T(8,128)(2,1)S(1)} %collective-permute-done.3.refs_3_), channel_id=1, source_target_pairs={{0,4},{1,5},{2,6},{3,7},{4,0},{5,1},{6,2},{7,3},{8,12},{9,13},{10,... | collective-permute-start | bytes 1572872 | tf_op jit(solution)/shard_map/ppermute | solution.py:47
  69.1 15.9 %collective-permute-start.23 = (bf16[256,1024]{1,0:T(8,128)(2,1)S(1)}, bf16[256,1024]{1,0:T(8,128)(2,1)S(1)}, u32[]{:S(2)}, u32[]{:S(2)}) collective-permute-start(bf16[256,1024]{1,0:T(8,128)(2,1)S(1)} %collective-permute-done.11.refs_11_), channel_id=1, source_target_pairs={{0,4},{1,5},{2,6},{3,7},{4,0},{5,1},{6,2},{7,3},{8,12},{9,13},{10,... | collective-permute-start | bytes 1572872 | tf_op jit(solution)/shard_map/ppermute | solution.py:47
  130.7 7.3 %collective-permute-start.25 = (f32[8,1024]{1,0:T(8,128)S(1)}, f32[8,1024]{1,0:T(8,128)S(1)}, u32[]{:S(2)}, u32[]{:S(2)}) collective-permute-start(f32[8,1024]{1,0:T(8,128)S(1)} %add.73), channel_id=1, source_target_pairs={{0,64},{32,96},{64,0},{96,32},{1,65},{33,97},{65,1},{97,33},{2,66}... | collective-permute-start | bytes 98312 | tf_op jit(solution)/shard_map/ppermute | solution.py:323
  131.3 6.7 %collective-permute-start.26 = (f32[8,1024]{1,0:T(8,128)S(1)}, f32[8,1024]{1,0:T(8,128)S(1)}, u32[]{:S(2)}, u32[]{:S(2)}) collective-permute-start(f32[8,1024]{1,0:T(8,128)S(1)} %add.73), channel_id=1, source_target_pairs={{0,32},{32,64},{64,96},{96,0},{1,33},{33,65},{65,97},{97,1},{2,34}... | collective-permute-start | bytes 98312 | tf_op jit(solution)/shard_map/ppermute | solution.py:323
  133.1 4.9 %collective-permute-start.27 = (f32[8,1024]{1,0:T(8,128)S(1)}, f32[8,1024]{1,0:T(8,128)S(1)}, u32[]{:S(2)}, u32[]{:S(2)}) collective-permute-start(f32[8,1024]{1,0:T(8,128)S(1)} %add.73), channel_id=1, source_target_pairs={{0,96},{32,0},{64,32},{96,64},{1,97},{33,1},{65,33},{97,65},{2,98}... | collective-permute-start | bytes 98312 | tf_op jit(solution)/shard_map/ppermute | solution.py:323
  134.5 21.2 %all-to-all-start.1 = ((f32[4,16,1536]{2,1,0:T(8,128)}), f32[4,16,1536]{2,1,0:T(8,128)S(1)}, u32[]{:S(2)}, u32[]{:S(2)}) async-start(f32[4,16,1536]{2,1,0:T(8,128)} %get-tuple-element.19), calls=%async_computation.1 | async-start | bytes 786432 | tf_op jit(solution)/shard_map/all_to_all | solution.py:358
  138.0 7.2 %collective-permute-start.28 = (f32[8,1024]{1,0:T(8,128)S(1)}, f32[8,1024]{1,0:T(8,128)S(1)}, u32[]{:S(2)}, u32[]{:S(2)}) collective-permute-start(f32[8,1024]{1,0:T(8,128)S(1)} %add_add_fusion.1), channel_id=1, source_target_pairs={{0,16},{8,24},{16,0},{24,8},{1,17},{9,25},{17,1},{25,9},{2,18},{10... | collective-permute-start | bytes 98312 | tf_op jit(solution)/shard_map/ppermute | solution.py:323
  142.0 5.1 %collective-permute-start.29 = (f32[8,1024]{1,0:T(8,128)S(1)}, f32[8,1024]{1,0:T(8,128)S(1)}, u32[]{:S(2)}, u32[]{:S(2)}) collective-permute-start(f32[8,1024]{1,0:T(8,128)S(1)} %add_add_fusion.1), channel_id=1, source_target_pairs={{0,8},{8,16},{16,24},{24,0},{1,9},{9,17},{17,25},{25,1},{2,10},{10... | collective-permute-start | bytes 98312 | tf_op jit(solution)/shard_map/ppermute | solution.py:323
  147.1 7.1 %collective-permute-start.31 = (f32[8,1024]{1,0:T(8,128)S(1)}, f32[8,1024]{1,0:T(8,128)S(1)}, u32[]{:S(2)}, u32[]{:S(2)}) collective-permute-start(f32[8,1024]{1,0:T(8,128)S(1)} %add_add_fusion.p0), channel_id=1, source_target_pairs={{0,1},{1,2},{2,3},{3,0},{4,5},{5,6},{6,7},{7,4},{8,9},{9,10},{10,1... | collective-permute-start | bytes 98312 | tf_op jit(solution)/shard_map/ppermute | solution.py:323
  149.2 5.4 %collective-permute-start.32 = (f32[8,1024]{1,0:T(8,128)S(1)}, f32[8,1024]{1,0:T(8,128)S(1)}, u32[]{:S(2)}, u32[]{:S(2)}) collective-permute-start(f32[8,1024]{1,0:T(8,128)S(1)} %add_add_fusion.p0), channel_id=1, source_target_pairs={{0,2},{1,3},{2,0},{3,1},{4,6},{5,7},{6,4},{7,5},{8,10},{9,11},{10,... | collective-permute-start | bytes 98312 | tf_op jit(solution)/shard_map/ppermute | solution.py:323
  (17 other events, 251.7 us)
where the time goes:
time: 158 us; the launch traced here: 157 us
  waiting for transfers between devices  45.8 us (29%)
  Pallas kernels  45.3 us (29%)
  starting transfers between devices  38.9 us (25%)
  blocking collectives  15.8 us (10%)
  local copies, waits for them, and re-layouts  9.75 us (6%)
    pallas_call x1, Pallas kernels, run_local(): pl.pallas_call(local_steps, out_shape=(jax.ShapeDtypeStruct((blocks, own,...  43.2 us
    ppermute x25, waiting for transfers between devices, send(): return lax.ppermute(value, ALL, perm)  42.4 us
    ppermute x25, starting transfers between devices, send(): return lax.ppermute(value, ALL, perm)  18.2 us
    ppermute x9, starting transfers between devices, shift(): return lax.ppermute(value, axis, [(i, (i + by) % n) for i in range(n)])  17.2 us
    all_to_all x1, blocking collectives, per_device(): state = lax.all_to_all(sent, 'y', 0, 0, tiled=True)  15.8 us
    unnamed x29, local copies, waits for them, and re-layouts  7.6 us
    all_to_all x1, starting transfers between devices, per_device(): back = lax.all_to_all(result, 'y', 0, 0, tiled=True)  3.46 us
    ppermute x9, waiting for transfers between devices, shift(): return lax.ppermute(value, axis, [(i, (i + by) % n) for i in range(n)])  3.41 us
  transfers between devices with their start and end apart: 35, of which 13 were waited for; matrix products, arithmetic and copies ran while one was open for 1% of the time, Pallas kernels for 0%

commit v1 on v0

--- a/solution.py
+++ b/solution.py
@@ -63,7 +63,7 @@
     up1, down1 = send(one, UP), send(one, DOWN)
     up3, down3 = send(three, UP), send(three, DOWN)
     up2, down2 = send(two, UP), send(two, DOWN)
-    far1 = send(up1, UP)
+    far1 = send(far, FIRST)
     far2 = send(far, SECOND)
     far3 = send(down3, DOWN)
     mine = [[one, up1, down1, far1], [two, up2, down2, far2], [three, up3, down3, far3]]
@@ -71,23 +71,24 @@
     return mine, theirs
 
 
-def prepare(place, cost_h, ph_h, start_h, consensus, upper, matrix, sent, far, cost, ph_mult, start, sem):
+def prepare(place, cost_h, ph_h, start_h, consensus, upper, matrix, kept, one, opposite, two, far, *scratch):
+    cost, ph_mult, start, sem = scratch
     loads = ((cost_h, cost), (ph_h, ph_mult), (start_h, start))
     loads += ((matrix.at[pl.ds(pl.multiple_of(place[3], TILE), TILE)], far),)
     copies = [pltpu.make_async_copy(src, dst, sem.at[k]) for k, (src, dst) in enumerate(loads)]
     for copy in copies:
         copy.start()
-    blocks, rows, width = sent.shape
+    rows, width = kept.shape
     own = (rows - 8) // 2
     flat = jnp.concatenate([upper[...], consensus[...], jnp.zeros((6, width), jnp.float32)], axis=0)
-    for b in range(blocks):
-        sent[b, 2 * own :] = flat
+    for sent in (kept, one, two, opposite):
+        sent[2 * own :] = flat
     for copy in copies[:3]:
         copy.wait()
-    for b in range(blocks):
-        at = slice(b * own, (b + 1) * own)
-        sent[b, :own] = cost[at] + ph_mult[at] - penalty * consensus[...]
-        sent[b, own : 2 * own] = start[at]
+    for slot, sent in enumerate((kept, one, two, opposite)):
+        at = pl.ds(pl.multiple_of(place[8 + slot] * own, own), own)
+        sent[:own] = cost[at] + ph_mult[at] - penalty * consensus[...]
+        sent[own : 2 * own] = start[at]
     copies[3].wait()
 
 
@@ -96,16 +97,14 @@
     vmem = pl.BlockSpec(memory_space=pltpu.VMEM)
     hbm = pl.BlockSpec(memory_space=pltpu.HBM)
     held = pltpu.VMEM((group, width), jnp.float32)
+    state = jax.ShapeDtypeStruct((2 * group // blocks + 8, width), jnp.float32)
     return pl.pallas_call(
         prepare,
-        out_shape=(
-            jax.ShapeDtypeStruct((blocks, 2 * group // blocks + 8, width), jnp.float32),
-            jax.ShapeDtypeStruct((TILE, width), jnp.bfloat16),
-        ),
+        out_shape=(state, state, state, state, jax.ShapeDtypeStruct((TILE, width), jnp.bfloat16)),
         in_specs=[pl.BlockSpec(memory_space=pltpu.SMEM)] + [hbm] * 3 + [vmem] * 2 + [hbm],
-        out_specs=(vmem, vmem),
+        out_specs=(vmem,) * 5,
         scratch_shapes=[held, held, held, pltpu.SemaphoreType.DMA((4,))],
-        compiler_params=pltpu.CompilerParams(vmem_limit_bytes=8 * 1024 * 1024),
+        compiler_params=pltpu.CompilerParams(vmem_limit_bytes=60 * 1024 * 1024),
         cost_estimate=pl.CostEstimate(
             flops=4000000, bytes_accessed=5 * group * width * 4, transcendentals=0
         ),
@@ -155,8 +154,9 @@
 
 def local_steps(place, *refs):
     pieces, refs = refs[:24], refs[24:]
-    own_a, scale_h, rhs_h, mult_h, weight_h, state, out, parts = refs[:8]
-    a_v, at_v, x_v, w_v, back_v, scale, rhs, mult, weight, sem, row_sem = refs[8:]
+    own_a, scale_h, rhs_h, mult_h, weight_h = refs[:5]
+    state, (out, parts, old) = refs[5:9], refs[9:12]
+    a_v, at_v, x_v, w_v, back_v, scale, rhs, mult, weight, sem, row_sem = refs[12:]
     slots, width = a_v.shape[1], a_v.shape[3]
     n_piece = a_v.shape[0]
     rows = n_piece * TILE
@@ -189,7 +189,8 @@
             pltpu.make_async_copy(piece, a_v.at[p, slot], sem.at[p]).start()
 
     for b in range(slots):
-        x_v[b] = state[place[8 + b], own : 2 * own]
+        x_v[b] = state[b][own : 2 * own]
+        old[pl.ds(place[8 + b], 1)] = state[b][2 * own + 1 : 2 * own + 2]
     for copy in waits:
         copy.wait()
 
@@ -223,10 +224,9 @@
                 )
 
     def move(b, col, back):
-        block = place[8 + b]
         x = x_v[b, :, col]
-        grad = state[block, :own, col] + penalty * x + back
-        box = state[block, 2 * own : 2 * own + 1, col]
+        grad = state[b][:own, col] + penalty * x + back
+        box = state[b][2 * own : 2 * own + 1, col]
         x_v[b, :, col] = jnp.clip(x - step_size * grad, -box, box)
 
     back_v[...] = jnp.zeros_like(back_v)
@@ -279,7 +279,7 @@
 
 def run_local(place, mine, theirs, matrix, scale, rhs, mult, weight, state):
     rows, width = matrix.shape
-    blocks = state.shape[0]
+    blocks = len(state)
     own = scale.shape[0] // blocks
     n_piece = rows // TILE
     pieces = [piece for block in mine + theirs for piece in block]
@@ -292,9 +292,10 @@
         out_shape=(
             jax.ShapeDtypeStruct((blocks, own, width + rows // blocks), jnp.float32),
             jax.ShapeDtypeStruct((8, width), jnp.float32),
+            jax.ShapeDtypeStruct((blocks, width), jnp.float32),
         ),
-        in_specs=[smem] + [hbm] * (len(pieces) + 5) + [vmem],
-        out_specs=(vmem, vmem),
+        in_specs=[smem] + [hbm] * (len(pieces) + 5) + [vmem] * blocks,
+        out_specs=(vmem,) * 3,
         scratch_shapes=[
             pltpu.VMEM((n_piece, blocks, TILE, width), jnp.bfloat16),
             pltpu.VMEM((blocks * width, rows), jnp.bfloat16),
@@ -308,14 +309,14 @@
             pltpu.SemaphoreType.DMA((n_piece,)),
             pltpu.SemaphoreType.DMA((3 * n_piece + 1,)),
         ],
-        compiler_params=pltpu.CompilerParams(vmem_limit_bytes=44 * 1024 * 1024),
+        compiler_params=pltpu.CompilerParams(vmem_limit_bytes=37 * 1024 * 1024),
         cost_estimate=pl.CostEstimate(
             flops=2 * (2 * ITERS + 1) * own * rows * blocks * width,
             bytes_accessed=2 * blocks * rows * width,
             transcendentals=0,
         ),
         name="local_steps",
-    )(place, *pieces, matrix, scale, rhs, mult, weight, state)
+    )(place, *pieces, matrix, scale, rhs, mult, weight, *state)
 
 
 def shift(value, axis, by):
@@ -346,12 +347,14 @@
             jnp.stack([me * own]),
         ]
     ).astype(jnp.int32)
-    sent, far = run_prepare(place, cost, ph_mult, start, consensus, upper, cons_matrix, blocks)
+    kept, first, opposite, second, far = run_prepare(
+        place, cost, ph_mult, start, consensus, upper, cons_matrix, blocks
+    )
     mine, theirs = gather_matrix(cons_matrix, far)
-    state = lax.all_to_all(sent, "y", 0, 0, tiled=True)
+    state = (kept, send(first, FIRST), send(second, SECOND), send(send(opposite, FIRST), SECOND))
 
     weight = jnp.broadcast_to(prob[:, None], (group, 128))
-    result, parts = run_local(
+    result, parts, old = run_local(
         place, mine, theirs, cons_matrix, row_scale, rhs, cons_mult, weight, state
     )
 
@@ -360,7 +363,7 @@
     parts = ring_sum(ring_sum(parts, "x"), "z")
     shares = (parts, shift(parts, "y", 1), shift(parts, "y", 2), shift(parts, "y", 3))
     x, mult_new, z_new, w_new, primal_res, dual_res = run_finish(
-        place, shares, back, ph_mult, state[:, 2 * own + 1]
+        place, shares, back, ph_mult, old
     )
     return (x, mult_new, z_new[0], w_new, primal_res[0, 0], dual_res[0, 0])
 

time: 158 us -> 160 us (1.013)
  blocking collectives: 15.8 us -> 0 us
  waiting for transfers between devices: 45.8 us -> 59.6 us
  starting transfers between devices: 38.9 us -> 47.6 us
  local copies, waits for them, and re-layouts: 9.75 us -> 2.75 us
  Pallas kernels: 45.3 us -> 47.2 us
    all_to_all x1 -> x0, blocking collectives: 15.8 us -> none  [per_device(): state = lax.all_to_all(sent, 'y', 0, 0, tiled=True)]
    ppermute x25 -> x29, starting transfers between devices: 18.2 us -> 28.4 us  [send(): return lax.ppermute(value, ALL, perm)]
    ppermute x25 -> x29, waiting for transfers between devices: 42.4 us -> 51.2 us  [send(): return lax.ppermute(value, ALL, perm)]
    unnamed x29 -> x14, local copies, waits for them, and re-layouts: 7.6 us -> 0.94 us
    ppermute x9, waiting for transfers between devices: 3.41 us -> 8.33 us  [shift(): return lax.ppermute(value, axis, [(i, (i + by) % n) for i in range(n)])]
    pallas_call x1, Pallas kernels: 0.73 us -> 3.07 us  [run_prepare(): pl.pallas_call(prepare, out_shape=(state, state, state, state, jax.ShapeD...]
  transfers between devices with their start and end apart: 35 -> 39, of which waited for: 13 -> 16; matrix products, arithmetic and copies ran while one was open for 1% -> 1% of each run, Pallas kernels for 0% -> 0%
where the time goes in v1:
time: 160 us; the launch traced here: 159 us
  waiting for transfers between devices  59.6 us (37%)
  starting transfers between devices  47.6 us (30%)
  Pallas kernels  47.2 us (30%)
  local copies, waits for them, and re-layouts  2.75 us (2%)
    ppermute x29, waiting for transfers between devices, send(): return lax.ppermute(value, ALL, perm)  51.2 us
    pallas_call x1, Pallas kernels, run_local(): pl.pallas_call(local_steps, out_shape=(jax.ShapeDtypeStruct((blocks, own,...  42.7 us
    ppermute x29, starting transfers between devices, send(): return lax.ppermute(value, ALL, perm)  28.4 us
    ppermute x9, starting transfers between devices, shift(): return lax.ppermute(value, axis, [(i, (i + by) % n) for i in range(n)])  15.7 us
    ppermute x9, waiting for transfers between devices, shift(): return lax.ppermute(value, axis, [(i, (i + by) % n) for i in range(n)])  8.33 us
    all_to_all x1, starting transfers between devices, per_device(): back = lax.all_to_all(result, 'y', 0, 0, tiled=True)  3.46 us
  transfers between devices with their start and end apart: 39, of which 16 were waited for; matrix products, arithmetic and copies ran while one was open for 1% of the time, Pallas kernels for 0%

profile of v1, /device:TPU:0, one launch (start us, length us, event | category | flops | bytes accessed | tf_op | source)
XLA Modules:
  0.0 158.7 jit_solution(5332635464306348452)
XLA Ops:
  2.1 3.1 %prepare.1 = (f32[40,1024]{1,0:T(8,128)}, f32[40,1024]{1,0:T(8,128)}, f32[40,1024]{1,0:T(8,128)}, f32[40,1024]{1,0:T(8,128)}, bf16[256,1024]{1,0:T(8,128)(2,1)}) custom-call(s32[13]{0:T(128)} %concatenate.3.place, f32[64,1024]{1,0:T(8,128)} %cost_h.1, f32[64,1024]{1,0:T(8,128)} %ph_mult.1, f32[64,1024]{1,0:T(8,128)} %start_h.1, f32[1,1024]{1,0:T(1,128)} %bitcast.10, ...), custom_call_target="tpu_custom_call" | custom-call | flops 4000000 | bytes 1310720 | tf_op jit(solution)/shard_map/prepare/pallas_call | solution.py:101
  5.2 1.8 %collective-permute-start.24 = (f32[40,1024]{1,0:T(8,128)}, f32[40,1024]{1,0:T(8,128)S(1)}, u32[]{:S(2)}, u32[]{:S(2)}) collective-permute-start(f32[40,1024]{1,0:T(8,128)} %get-tuple-element.22), channel_id=1, source_target_pairs={{0,1},{1,0},{2,3},{3,2},{4,7},{5,6},{6,5},{7,4},{8,9},{9,8},{10,11... | collective-permute-start | bytes 491528 | tf_op jit(solution)/shard_map/ppermute | solution.py:47
  8.1 2.3 %collective-permute-start.4 = (bf16[256,1024]{1,0:T(8,128)(2,1)S(1)}, bf16[256,1024]{1,0:T(8,128)(2,1)S(1)}, u32[]{:S(2)}, u32[]{:S(2)}) collective-permute-start(bf16[256,1024]{1,0:T(8,128)(2,1)S(1)} %constant_dynamic-slice_fusion), channel_id=1, source_target_pairs={{0,3},{1,2},{2,1},{3,0},{4,5},{5,4},{6,7},{7,6},{8,11},{9,10},{10,... | collective-permute-start | bytes 1572872 | tf_op jit(solution)/shard_map/ppermute | solution.py:47
  11.7 1.1 collective-permute-start.3
  12.8 2.9 %collective-permute-start.25 = (f32[40,1024]{1,0:T(8,128)}, f32[40,1024]{1,0:T(8,128)S(1)}, u32[]{:S(2)}, u32[]{:S(2)}) collective-permute-start(f32[40,1024]{1,0:T(8,128)} %get-tuple-element.23), channel_id=1, source_target_pairs={{0,3},{1,2},{2,1},{3,0},{4,5},{5,4},{6,7},{7,6},{8,11},{9,10},{10,... | collective-permute-start | bytes 491528 | tf_op jit(solution)/shard_map/ppermute | solution.py:47
  15.7 21.4 %collective-permute-done.25.refs_31_ = f32[40,1024]{1,0:T(8,128)S(1)} collective-permute-done((f32[40,1024]{1,0:T(8,128)}, f32[40,1024]{1,0:T(8,128)S(1)}, u32[]{:S(2)}, u32[]{:S(2)}) %collective-permute-start.25) | collective-permute-done | bytes 163872 | tf_op jit(solution)/shard_map/ppermute | solution.py:47
  37.2 5.5 %collective-permute-done.26 = f32[40,1024]{1,0:T(8,128)S(1)} collective-permute-done((f32[40,1024]{1,0:T(8,128)}, f32[40,1024]{1,0:T(8,128)S(1)}, u32[]{:S(2)}, u32[]{:S(2)}) %collective-permute-start.26) | collective-permute-done | bytes 163872 | tf_op jit(solution)/shard_map/ppermute | solution.py:47
  42.7 1.1 collective-permute-start.27
  43.8 5.4 %collective-permute-done.27.refs_32_ = f32[40,1024]{1,0:T(8,128)S(1)} collective-permute-done((f32[40,1024]{1,0:T(8,128)S(1)}, f32[40,1024]{1,0:T(8,128)S(1)}, u32[]{:S(2)}, u32[]{:S(2)}) %collective-permute-start.27) | collective-permute-done | bytes 163872 | tf_op jit(solution)/shard_map/ppermute | solution.py:47
  49.2 2.8 %collective-permute-start.6 = (bf16[256,1024]{1,0:T(8,128)(2,1)S(1)}, bf16[256,1024]{1,0:T(8,128)(2,1)S(1)}, u32[]{:S(2)}, u32[]{:S(2)}) collective-permute-start(bf16[256,1024]{1,0:T(8,128)(2,1)S(1)} %collective-permute-done.4.refs_4_), channel_id=1, source_target_pairs={{0,96},{1,97},{2,98},{3,99},{4,28},{5,29},{6,30},{7,31},{8,104},{9... | collective-permute-start | bytes 1572872 | tf_op jit(solution)/shard_map/ppermute | solution.py:47
  52.1 1.2 collective-permute-start.8
  53.3 3.1 %collective-permute-start.2 = (bf16[256,1024]{1,0:T(8,128)(2,1)S(1)}, bf16[256,1024]{1,0:T(8,128)(2,1)S(1)}, u32[]{:S(2)}, u32[]{:S(2)}) collective-permute-start(bf16[256,1024]{1,0:T(8,128)(2,1)S(1)} %collective-permute-done.refs_0_), channel_id=1, source_target_pairs={{0,96},{1,97},{2,98},{3,99},{4,28},{5,29},{6,30},{7,31},{8,104},{9... | collective-permute-start | bytes 1572872 | tf_op jit(solution)/shard_map/ppermute | solution.py:47
  56.4 2.3 %collective-permute-done.6.refs_6_ = bf16[256,1024]{1,0:T(8,128)(2,1)S(1)} collective-permute-done((bf16[256,1024]{1,0:T(8,128)(2,1)S(1)}, bf16[256,1024]{1,0:T(8,128)(2,1)S(1)}, u32[]{:S(2)}, u32[]{:S(2)}) %collective-permute-start.6) | collective-permute-done | bytes 524320 | tf_op jit(solution)/shard_map/ppermute | solution.py:47
  58.7 1.2 collective-permute-start.1
  59.9 2.5 %collective-permute-done.5.refs_5_ = bf16[256,1024]{1,0:T(8,128)(2,1)S(1)} collective-permute-done((bf16[256,1024]{1,0:T(8,128)(2,1)S(1)}, bf16[256,1024]{1,0:T(8,128)(2,1)S(1)}, u32[]{:S(2)}, u32[]{:S(2)}) %collective-permute-start.5) | collective-permute-done | bytes 524320 | tf_op jit(solution)/shard_map/ppermute | solution.py:47
  62.9 2.8 %collective-permute-start.10 = (bf16[256,1024]{1,0:T(8,128)(2,1)S(1)}, bf16[256,1024]{1,0:T(8,128)(2,1)S(1)}, u32[]{:S(2)}, u32[]{:S(2)}) collective-permute-start(bf16[256,1024]{1,0:T(8,128)(2,1)S(1)} %collective-permute-done.8.refs_8_), channel_id=1, source_target_pairs={{0,96},{1,97},{2,98},{3,99},{4,28},{5,29},{6,30},{7,31},{8,104},{9... | collective-permute-start | bytes 1572872 | tf_op jit(solution)/shard_map/ppermute | solution.py:47
  66.7 2.8 %collective-permute-done.1.refs_1_ = bf16[256,1024]{1,0:T(8,128)(2,1)S(1)} collective-permute-done((bf16[256,1024]{1,0:T(8,128)(2,1)S(1)}, bf16[256,1024]{1,0:T(8,128)(2,1)S(1)}, u32[]{:S(2)}, u32[]{:S(2)}) %collective-permute-start.1) | collective-permute-done | bytes 524320 | tf_op jit(solution)/shard_map/ppermute | solution.py:47
  70.0 2.4 %collective-permute-done.10.refs_10_ = bf16[256,1024]{1,0:T(8,128)(2,1)S(1)} collective-permute-done((bf16[256,1024]{1,0:T(8,128)(2,1)S(1)}, bf16[256,1024]{1,0:T(8,128)(2,1)S(1)}, u32[]{:S(2)}, u32[]{:S(2)}) %collective-permute-start.10) | collective-permute-done | bytes 524320 | tf_op jit(solution)/shard_map/ppermute | solution.py:47
  72.4 3.7 %collective-permute-start.11 = (bf16[256,1024]{1,0:T(8,128)(2,1)S(1)}, bf16[256,1024]{1,0:T(8,128)(2,1)S(1)}, u32[]{:S(2)}, u32[]{:S(2)}) collective-permute-start(bf16[256,1024]{1,0:T(8,128)(2,1)S(1)} %collective-permute-done.10.refs_10_), channel_id=1, source_target_pairs={{0,96},{1,97},{2,98},{3,99},{4,28},{5,29},{6,30},{7,31},{8,104},{9... | collective-permute-start | bytes 1572872 | tf_op jit(solution)/shard_map/ppermute | solution.py:47
  76.7 3.7 %collective-permute-done.9.refs_9_ = bf16[256,1024]{1,0:T(8,128)(2,1)S(1)} collective-permute-done((bf16[256,1024]{1,0:T(8,128)(2,1)S(1)}, bf16[256,1024]{1,0:T(8,128)(2,1)S(1)}, u32[]{:S(2)}, u32[]{:S(2)}) %collective-permute-start.9) | collective-permute-done | bytes 524320 | tf_op jit(solution)/shard_map/ppermute | solution.py:47
  80.5 2.2 %collective-permute-done.11.refs_11_ = bf16[256,1024]{1,0:T(8,128)(2,1)S(1)} collective-permute-done((bf16[256,1024]{1,0:T(8,128)(2,1)S(1)}, bf16[256,1024]{1,0:T(8,128)(2,1)S(1)}, u32[]{:S(2)}, u32[]{:S(2)}) %collective-permute-start.11) | collective-permute-done | bytes 524320 | tf_op jit(solution)/shard_map/ppermute | solution.py:47
  82.8 1.9 %collective-permute-done.23.refs_23_ = bf16[256,1024]{1,0:T(8,128)(2,1)S(1)} collective-permute-done((bf16[256,1024]{1,0:T(8,128)(2,1)S(1)}, bf16[256,1024]{1,0:T(8,128)(2,1)S(1)}, u32[]{:S(2)}, u32[]{:S(2)}) %collective-permute-start.23) | collective-permute-done | bytes 524320 | tf_op jit(solution)/shard_map/ppermute | solution.py:47
  85.7 42.7 %local_steps.1 = (f32[4,16,1536]{2,1,0:T(8,128)}, f32[8,1024]{1,0:T(8,128)S(1)}, f32[4,1024]{1,0:T(4,128)S(1)}) custom-call(s32[13]{0:T(128)S(1)} %copy-done.5, bf16[256,1024]{1,0:T(8,128)(2,1)S(1)} %collective-permute-done.refs_0_, bf16[256,1024]{1,0:T(8,128)(2,1)S(1)} %collective-permute-done.1.refs_1_, ...), custom_call_target="tpu_custom_call" | custom-call | flops 4563402752 | bytes 16777216 | tf_op jit(solution)/shard_map/local_steps/pallas_call | solution.py:290
  129.7 3.7 %collective-permute-start.31 = (f32[8,1024]{1,0:T(8,128)S(1)}, f32[8,1024]{1,0:T(8,128)S(1)}, u32[]{:S(2)}, u32[]{:S(2)}) collective-permute-start(f32[8,1024]{1,0:T(8,128)S(1)} %add.73), channel_id=1, source_target_pairs={{0,96},{32,0},{64,32},{96,64},{1,97},{33,1},{65,33},{97,65},{2,98}... | collective-permute-start | bytes 98312 | tf_op jit(solution)/shard_map/ppermute | solution.py:324
  133.4 1.5 collective-permute-start.29
  135.0 3.5 %all-to-all-start = ((f32[4,16,1536]{2,1,0:T(8,128)}), f32[4,16,1536]{2,1,0:T(8,128)S(1)}, u32[]{:S(2)}, u32[]{:S(2)}) async-start(f32[4,16,1536]{2,1,0:T(8,128)} %get-tuple-element.26), calls=%async_computation | async-start | bytes 786432 | tf_op jit(solution)/shard_map/all_to_all | solution.py:361
  138.9 4.1 %collective-permute-start.34 = (f32[8,1024]{1,0:T(8,128)S(1)}, f32[8,1024]{1,0:T(8,128)S(1)}, u32[]{:S(2)}, u32[]{:S(2)}) collective-permute-start(f32[8,1024]{1,0:T(8,128)S(1)} %add_add_fusion.1), channel_id=1, source_target_pairs={{0,24},{8,0},{16,8},{24,16},{1,25},{9,1},{17,9},{25,17},{2,26},{10... | collective-permute-start | bytes 98312 | tf_op jit(solution)/shard_map/ppermute | solution.py:324
  143.0 1.9 %collective-permute-start.32 = (f32[8,1024]{1,0:T(8,128)S(1)}, f32[8,1024]{1,0:T(8,128)S(1)}, u32[]{:S(2)}, u32[]{:S(2)}) collective-permute-start(f32[8,1024]{1,0:T(8,128)S(1)} %add_add_fusion.1), channel_id=1, source_target_pairs={{0,16},{8,24},{16,0},{24,8},{1,17},{9,25},{17,1},{25,9},{2,18},{10... | collective-permute-start | bytes 98312 | tf_op jit(solution)/shard_map/ppermute | solution.py:324
  144.9 3.3 %collective-permute-done.33 = f32[8,1024]{1,0:T(8,128)S(1)} collective-permute-done((f32[8,1024]{1,0:T(8,128)S(1)}, f32[8,1024]{1,0:T(8,128)S(1)}, u32[]{:S(2)}, u32[]{:S(2)}) %collective-permute-start.33) | collective-permute-done | bytes 32800 | tf_op jit(solution)/shard_map/ppermute | solution.py:324
  148.5 2.8 %collective-permute-start.37 = (f32[8,1024]{1,0:T(8,128)S(1)}, f32[8,1024]{1,0:T(8,128)S(1)}, u32[]{:S(2)}, u32[]{:S(2)}) collective-permute-start(f32[8,1024]{1,0:T(8,128)S(1)} %add_add_fusion.p0), channel_id=1, source_target_pairs={{0,3},{1,0},{2,1},{3,2},{4,7},{5,4},{6,5},{7,6},{8,11},{9,8},{10,9... | collective-permute-start | bytes 98312 | tf_op jit(solution)/shard_map/ppermute | solution.py:324
  153.0 3.7 %collective-permute-done.36.p2 = f32[8,1024]{1,0:T(8,128)S(1)} collective-permute-done((f32[8,1024]{1,0:T(8,128)S(1)}, f32[8,1024]{1,0:T(8,128)S(1)}, u32[]{:S(2)}, u32[]{:S(2)}) %collective-permute-start.36) | collective-permute-done | bytes 32800 | tf_op jit(solution)/shard_map/ppermute | solution.py:324
  157.3 1.4 finish.1
  (70 shorter events, 12.2 us)
Async XLA Ops:
  5.2 7.6 %collective-permute-start.24 = (f32[40,1024]{1,0:T(8,128)}, f32[40,1024]{1,0:T(8,128)S(1)}, u32[]{:S(2)}, u32[]{:S(2)}) collective-permute-start(f32[40,1024]{1,0:T(8,128)} %get-tuple-element.22), channel_id=1, source_target_pairs={{0,1},{1,0},{2,3},{3,2},{4,7},{5,6},{6,5},{7,4},{8,9},{9,8},{10,11... | collective-permute-start | bytes 491528 | tf_op jit(solution)/shard_map/ppermute | solution.py:47
  8.1 35.7 %collective-permute-start.4 = (bf16[256,1024]{1,0:T(8,128)(2,1)S(1)}, bf16[256,1024]{1,0:T(8,128)(2,1)S(1)}, u32[]{:S(2)}, u32[]{:S(2)}) collective-permute-start(bf16[256,1024]{1,0:T(8,128)(2,1)S(1)} %constant_dynamic-slice_fusion), channel_id=1, source_target_pairs={{0,3},{1,2},{2,1},{3,0},{4,5},{5,4},{6,7},{7,6},{8,11},{9,10},{10,... | collective-permute-start | bytes 1572872 | tf_op jit(solution)/shard_map/ppermute | solution.py:47
  10.3 41.6 %collective-permute-start = (bf16[256,1024]{1,0:T(8,128)(2,1)S(1)}, bf16[256,1024]{1,0:T(8,128)(2,1)S(1)}, u32[]{:S(2)}, u32[]{:S(2)}) collective-permute-start(bf16[256,1024]{1,0:T(8,128)(2,1)S(1)} %constant_dynamic-slice_fusion), channel_id=1, source_target_pairs={{0,1},{1,0},{2,3},{3,2},{4,7},{5,6},{6,5},{7,4},{8,9},{9,8},{10,11... | collective-permute-start | bytes 1572872 | tf_op jit(solution)/shard_map/ppermute | solution.py:47
  11.0 41.0 %collective-permute-start.7 = (bf16[256,1024]{1,0:T(8,128)(2,1)}, bf16[256,1024]{1,0:T(8,128)(2,1)S(1)}, u32[]{:S(2)}, u32[]{:S(2)}) collective-permute-start(bf16[256,1024]{1,0:T(8,128)(2,1)} %get-tuple-element.20), channel_id=1, source_target_pairs={{0,3},{1,2},{2,1},{3,0},{4,5},{5,4},{6,7},{7,6},{8,11},{9,10},{10,... | collective-permute-start | bytes 1572872 | tf_op jit(solution)/shard_map/ppermute | solution.py:47
  11.7 40.4 %collective-permute-start.3 = (bf16[256,1024]{1,0:T(8,128)(2,1)}, bf16[256,1024]{1,0:T(8,128)(2,1)S(1)}, u32[]{:S(2)}, u32[]{:S(2)}) collective-permute-start(bf16[256,1024]{1,0:T(8,128)(2,1)} %get-tuple-element.20), channel_id=1, source_target_pairs={{0,1},{1,0},{2,3},{3,2},{4,7},{5,6},{6,5},{7,4},{8,9},{9,8},{10,11... | collective-permute-start | bytes 1572872 | tf_op jit(solution)/shard_map/ppermute | solution.py:47
  12.8 24.3 %collective-permute-start.25 = (f32[40,1024]{1,0:T(8,128)}, f32[40,1024]{1,0:T(8,128)S(1)}, u32[]{:S(2)}, u32[]{:S(2)}) collective-permute-start(f32[40,1024]{1,0:T(8,128)} %get-tuple-element.23), channel_id=1, source_target_pairs={{0,3},{1,2},{2,1},{3,0},{4,5},{5,4},{6,7},{7,6},{8,11},{9,10},{10,... | collective-permute-start | bytes 491528 | tf_op jit(solution)/shard_map/ppermute | solution.py:47
  37.2 5.5 %collective-permute-start.26 = (f32[40,1024]{1,0:T(8,128)}, f32[40,1024]{1,0:T(8,128)S(1)}, u32[]{:S(2)}, u32[]{:S(2)}) collective-permute-start(f32[40,1024]{1,0:T(8,128)} %get-tuple-element.24), channel_id=1, source_target_pairs={{0,1},{1,0},{2,3},{3,2},{4,7},{5,6},{6,5},{7,4},{8,9},{9,8},{10,11... | collective-permute-start | bytes 491528 | tf_op jit(solution)/shard_map/ppermute | solution.py:47
  42.7 6.5 %collective-permute-start.27 = (f32[40,1024]{1,0:T(8,128)S(1)}, f32[40,1024]{1,0:T(8,128)S(1)}, u32[]{:S(2)}, u32[]{:S(2)}) collective-permute-start(f32[40,1024]{1,0:T(8,128)S(1)} %collective-permute-done.26), channel_id=1, source_target_pairs={{0,3},{1,2},{2,1},{3,0},{4,5},{5,4},{6,7},{7,6},{8,11},{9,10},{10,... | collective-permute-start | bytes 491528 | tf_op jit(solution)/shard_map/ppermute | solution.py:47
  43.8 9.5 %collective-permute-start.16 = (bf16[256,1024]{1,0:T(8,128)(2,1)S(1)}, bf16[256,1024]{1,0:T(8,128)(2,1)S(1)}, u32[]{:S(2)}, u32[]{:S(2)}) collective-permute-start(bf16[256,1024]{1,0:T(8,128)(2,1)S(1)} %collective-permute-done.4.refs_4_), channel_id=1, source_target_pairs={{0,4},{1,5},{2,6},{3,7},{4,0},{5,1},{6,2},{7,3},{8,12},{9,13},{10,... | collective-permute-start | bytes 1572872 | tf_op jit(solution)/shard_map/ppermute | solution.py:47
  49.2 9.5 %collective-permute-start.6 = (bf16[256,1024]{1,0:T(8,128)(2,1)S(1)}, bf16[256,1024]{1,0:T(8,128)(2,1)S(1)}, u32[]{:S(2)}, u32[]{:S(2)}) collective-permute-start(bf16[256,1024]{1,0:T(8,128)(2,1)S(1)} %collective-permute-done.4.refs_4_), channel_id=1, source_target_pairs={{0,96},{1,97},{2,98},{3,99},{4,28},{5,29},{6,30},{7,31},{8,104},{9... | collective-permute-start | bytes 1572872 | tf_op jit(solution)/shard_map/ppermute | solution.py:47
  52.0 10.4 %collective-permute-start.5 = (bf16[256,1024]{1,0:T(8,128)(2,1)S(1)}, bf16[256,1024]{1,0:T(8,128)(2,1)S(1)}, u32[]{:S(2)}, u32[]{:S(2)}) collective-permute-start(bf16[256,1024]{1,0:T(8,128)(2,1)S(1)} %collective-permute-done.4.refs_4_), channel_id=1, source_target_pairs={{0,32},{1,33},{2,34},{3,35},{4,12},{5,13},{6,14},{7,15},{8,40},{9,... | collective-permute-start | bytes 1572872 | tf_op jit(solution)/shard_map/ppermute | solution.py:47
  52.0 10.4 %collective-permute-start.12 = (bf16[256,1024]{1,0:T(8,128)(2,1)S(1)}, bf16[256,1024]{1,0:T(8,128)(2,1)S(1)}, u32[]{:S(2)}, u32[]{:S(2)}) collective-permute-start(bf16[256,1024]{1,0:T(8,128)(2,1)S(1)} %collective-permute-done.refs_0_), channel_id=1, source_target_pairs={{0,4},{1,5},{2,6},{3,7},{4,0},{5,1},{6,2},{7,3},{8,12},{9,13},{10,... | collective-permute-start | bytes 1572872 | tf_op jit(solution)/shard_map/ppermute | solution.py:47
  52.1 10.8 %collective-permute-start.8 = (bf16[256,1024]{1,0:T(8,128)(2,1)S(1)}, bf16[256,1024]{1,0:T(8,128)(2,1)S(1)}, u32[]{:S(2)}, u32[]{:S(2)}) collective-permute-start(bf16[256,1024]{1,0:T(8,128)(2,1)S(1)} %collective-permute-done.refs_0_), channel_id=1, source_target_pairs={{0,3},{1,2},{2,1},{3,0},{4,5},{5,4},{6,7},{7,6},{8,11},{9,10},{10,... | collective-permute-start | bytes 1572872 | tf_op jit(solution)/shard_map/ppermute | solution.py:47
  53.3 12.4 %collective-permute-start.2 = (bf16[256,1024]{1,0:T(8,128)(2,1)S(1)}, bf16[256,1024]{1,0:T(8,128)(2,1)S(1)}, u32[]{:S(2)}, u32[]{:S(2)}) collective-permute-start(bf16[256,1024]{1,0:T(8,128)(2,1)S(1)} %collective-permute-done.refs_0_), channel_id=1, source_target_pairs={{0,96},{1,97},{2,98},{3,99},{4,28},{5,29},{6,30},{7,31},{8,104},{9... | collective-permute-start | bytes 1572872 | tf_op jit(solution)/shard_map/ppermute | solution.py:47
  58.7 10.8 %collective-permute-start.1 = (bf16[256,1024]{1,0:T(8,128)(2,1)S(1)}, bf16[256,1024]{1,0:T(8,128)(2,1)S(1)}, u32[]{:S(2)}, u32[]{:S(2)}) collective-permute-start(bf16[256,1024]{1,0:T(8,128)(2,1)S(1)} %collective-permute-done.refs_0_), channel_id=1, source_target_pairs={{0,32},{1,33},{2,34},{3,35},{4,12},{5,13},{6,14},{7,15},{8,40},{9,... | collective-permute-start | bytes 1572872 | tf_op jit(solution)/shard_map/ppermute | solution.py:47
  62.4 7.2 %collective-permute-start.19 = (bf16[256,1024]{1,0:T(8,128)(2,1)S(1)}, bf16[256,1024]{1,0:T(8,128)(2,1)S(1)}, u32[]{:S(2)}, u32[]{:S(2)}) collective-permute-start(bf16[256,1024]{1,0:T(8,128)(2,1)S(1)} %collective-permute-done.7.refs_7_), channel_id=1, source_target_pairs={{0,4},{1,5},{2,6},{3,7},{4,0},{5,1},{6,2},{7,3},{8,12},{9,13},{10,... | collective-permute-start | bytes 1572872 | tf_op jit(solution)/shard_map/ppermute | solution.py:47
  62.4 7.7 %collective-permute-start.15 = (bf16[256,1024]{1,0:T(8,128)(2,1)S(1)}, bf16[256,1024]{1,0:T(8,128)(2,1)S(1)}, u32[]{:S(2)}, u32[]{:S(2)}) collective-permute-start(bf16[256,1024]{1,0:T(8,128)(2,1)S(1)} %collective-permute-done.3.refs_3_), channel_id=1, source_target_pairs={{0,4},{1,5},{2,6},{3,7},{4,0},{5,1},{6,2},{7,3},{8,12},{9,13},{10,... | collective-permute-start | bytes 1572872 | tf_op jit(solution)/shard_map/ppermute | solution.py:47
  62.9 9.5 %collective-permute-start.10 = (bf16[256,1024]{1,0:T(8,128)(2,1)S(1)}, bf16[256,1024]{1,0:T(8,128)(2,1)S(1)}, u32[]{:S(2)}, u32[]{:S(2)}) collective-permute-start(bf16[256,1024]{1,0:T(8,128)(2,1)S(1)} %collective-permute-done.8.refs_8_), channel_id=1, source_target_pairs={{0,96},{1,97},{2,98},{3,99},{4,28},{5,29},{6,30},{7,31},{8,104},{9... | collective-permute-start | bytes 1572872 | tf_op jit(solution)/shard_map/ppermute | solution.py:47
  65.7 10.4 %collective-permute-start.18 = (bf16[256,1024]{1,0:T(8,128)(2,1)S(1)}, bf16[256,1024]{1,0:T(8,128)(2,1)S(1)}, u32[]{:S(2)}, u32[]{:S(2)}) collective-permute-start(bf16[256,1024]{1,0:T(8,128)(2,1)S(1)} %collective-permute-done.6.refs_6_), channel_id=1, source_target_pairs={{0,4},{1,5},{2,6},{3,7},{4,0},{5,1},{6,2},{7,3},{8,12},{9,13},{10,... | collective-permute-start | bytes 1572872 | tf_op jit(solution)/shard_map/ppermute | solution.py:47
  69.5 6.6 %collective-permute-start.17 = (bf16[256,1024]{1,0:T(8,128)(2,1)S(1)}, bf16[256,1024]{1,0:T(8,128)(2,1)S(1)}, u32[]{:S(2)}, u32[]{:S(2)}) collective-permute-start(bf16[256,1024]{1,0:T(8,128)(2,1)S(1)} %collective-permute-done.5.refs_5_), channel_id=1, source_target_pairs={{0,4},{1,5},{2,6},{3,7},{4,0},{5,1},{6,2},{7,3},{8,12},{9,13},{10,... | collective-permute-start | bytes 1572872 | tf_op jit(solution)/shard_map/ppermute | solution.py:47
  69.5 7.1 %collective-permute-start.20 = (bf16[256,1024]{1,0:T(8,128)(2,1)S(1)}, bf16[256,1024]{1,0:T(8,128)(2,1)S(1)}, u32[]{:S(2)}, u32[]{:S(2)}) collective-permute-start(bf16[256,1024]{1,0:T(8,128)(2,1)S(1)} %collective-permute-done.8.refs_8_), channel_id=1, source_target_pairs={{0,4},{1,5},{2,6},{3,7},{4,0},{5,1},{6,2},{7,3},{8,12},{9,13},{10,... | collective-permute-start | bytes 1572872 | tf_op jit(solution)/shard_map/ppermute | solution.py:47
  70.0 10.4 %collective-permute-start.9 = (bf16[256,1024]{1,0:T(8,128)(2,1)S(1)}, bf16[256,1024]{1,0:T(8,128)(2,1)S(1)}, u32[]{:S(2)}, u32[]{:S(2)}) collective-permute-start(bf16[256,1024]{1,0:T(8,128)(2,1)S(1)} %collective-permute-done.8.refs_8_), channel_id=1, source_target_pairs={{0,32},{1,33},{2,34},{3,35},{4,12},{5,13},{6,14},{7,15},{8,40},{9,... | collective-permute-start | bytes 1572872 | tf_op jit(solution)/shard_map/ppermute | solution.py:47
  72.4 10.4 %collective-permute-start.11 = (bf16[256,1024]{1,0:T(8,128)(2,1)S(1)}, bf16[256,1024]{1,0:T(8,128)(2,1)S(1)}, u32[]{:S(2)}, u32[]{:S(2)}) collective-permute-start(bf16[256,1024]{1,0:T(8,128)(2,1)S(1)} %collective-permute-done.10.refs_10_), channel_id=1, source_target_pairs={{0,96},{1,97},{2,98},{3,99},{4,28},{5,29},{6,30},{7,31},{8,104},{9... | collective-permute-start | bytes 1572872 | tf_op jit(solution)/shard_map/ppermute | solution.py:47
  76.1 6.7 %collective-permute-start.14 = (bf16[256,1024]{1,0:T(8,128)(2,1)S(1)}, bf16[256,1024]{1,0:T(8,128)(2,1)S(1)}, u32[]{:S(2)}, u32[]{:S(2)}) collective-permute-start(bf16[256,1024]{1,0:T(8,128)(2,1)S(1)} %collective-permute-done.2.refs_2_), channel_id=1, source_target_pairs={{0,4},{1,5},{2,6},{3,7},{4,0},{5,1},{6,2},{7,3},{8,12},{9,13},{10,... | collective-permute-start | bytes 1572872 | tf_op jit(solution)/shard_map/ppermute | solution.py:47
  76.1 6.7 %collective-permute-start.13 = (bf16[256,1024]{1,0:T(8,128)(2,1)S(1)}, bf16[256,1024]{1,0:T(8,128)(2,1)S(1)}, u32[]{:S(2)}, u32[]{:S(2)}) collective-permute-start(bf16[256,1024]{1,0:T(8,128)(2,1)S(1)} %collective-permute-done.1.refs_1_), channel_id=1, source_target_pairs={{0,4},{1,5},{2,6},{3,7},{4,0},{5,1},{6,2},{7,3},{8,12},{9,13},{10,... | collective-permute-start | bytes 1572872 | tf_op jit(solution)/shard_map/ppermute | solution.py:47
  76.6 6.2 %collective-permute-start.22 = (bf16[256,1024]{1,0:T(8,128)(2,1)S(1)}, bf16[256,1024]{1,0:T(8,128)(2,1)S(1)}, u32[]{:S(2)}, u32[]{:S(2)}) collective-permute-start(bf16[256,1024]{1,0:T(8,128)(2,1)S(1)} %collective-permute-done.10.refs_10_), channel_id=1, source_target_pairs={{0,4},{1,5},{2,6},{3,7},{4,0},{5,1},{6,2},{7,3},{8,12},{9,13},{10,... | collective-permute-start | bytes 1572872 | tf_op jit(solution)/shard_map/ppermute | solution.py:47
  129.7 8.7 %collective-permute-start.31 = (f32[8,1024]{1,0:T(8,128)S(1)}, f32[8,1024]{1,0:T(8,128)S(1)}, u32[]{:S(2)}, u32[]{:S(2)}) collective-permute-start(f32[8,1024]{1,0:T(8,128)S(1)} %add.73), channel_id=1, source_target_pairs={{0,96},{32,0},{64,32},{96,64},{1,97},{33,1},{65,33},{97,65},{2,98}... | collective-permute-start | bytes 98312 | tf_op jit(solution)/shard_map/ppermute | solution.py:324
  133.4 5.5 %collective-permute-start.30 = (f32[8,1024]{1,0:T(8,128)S(1)}, f32[8,1024]{1,0:T(8,128)S(1)}, u32[]{:S(2)}, u32[]{:S(2)}) collective-permute-start(f32[8,1024]{1,0:T(8,128)S(1)} %add.73), channel_id=1, source_target_pairs={{0,32},{32,64},{64,96},{96,0},{1,33},{33,65},{65,97},{97,1},{2,34}... | collective-permute-start | bytes 98312 | tf_op jit(solution)/shard_map/ppermute | solution.py:324
  133.4 5.5 %collective-permute-start.29 = (f32[8,1024]{1,0:T(8,128)S(1)}, f32[8,1024]{1,0:T(8,128)S(1)}, u32[]{:S(2)}, u32[]{:S(2)}) collective-permute-start(f32[8,1024]{1,0:T(8,128)S(1)} %add.73), channel_id=1, source_target_pairs={{0,64},{32,96},{64,0},{96,32},{1,65},{33,97},{65,1},{97,33},{2,66}... | collective-permute-start | bytes 98312 | tf_op jit(solution)/shard_map/ppermute | solution.py:324
  135.0 22.3 %all-to-all-start = ((f32[4,16,1536]{2,1,0:T(8,128)}), f32[4,16,1536]{2,1,0:T(8,128)S(1)}, u32[]{:S(2)}, u32[]{:S(2)}) async-start(f32[4,16,1536]{2,1,0:T(8,128)} %get-tuple-element.26), calls=%async_computation | async-start | bytes 786432 | tf_op jit(solution)/shard_map/all_to_all | solution.py:361
  138.9 6.0 %collective-permute-start.34 = (f32[8,1024]{1,0:T(8,128)S(1)}, f32[8,1024]{1,0:T(8,128)S(1)}, u32[]{:S(2)}, u32[]{:S(2)}) collective-permute-start(f32[8,1024]{1,0:T(8,128)S(1)} %add_add_fusion.1), channel_id=1, source_target_pairs={{0,24},{8,0},{16,8},{24,16},{1,25},{9,1},{17,9},{25,17},{2,26},{10... | collective-permute-start | bytes 98312 | tf_op jit(solution)/shard_map/ppermute | solution.py:324
  143.0 5.5 %collective-permute-start.32 = (f32[8,1024]{1,0:T(8,128)S(1)}, f32[8,1024]{1,0:T(8,128)S(1)}, u32[]{:S(2)}, u32[]{:S(2)}) collective-permute-start(f32[8,1024]{1,0:T(8,128)S(1)} %add_add_fusion.1), channel_id=1, source_target_pairs={{0,16},{8,24},{16,0},{24,8},{1,17},{9,25},{17,1},{25,9},{2,18},{10... | collective-permute-start | bytes 98312 | tf_op jit(solution)/shard_map/ppermute | solution.py:324
  (14 other events, 517.4 us)
